TPU v7x, 512 devices: a whole 4x4x16 slice. The times are simulated.
512 devices in a mesh: sp: 8 (over z_hi, core), py: 16 (over z_lo, x), pz: 4 (over y).
Axes of the slice: x: 4, y: 4, z: 16 (z_hi: 4, z_lo: 4; z = z_hi * 4 + z_lo), core: 2. Of those that a mesh axis runs over, the one named last changes fastest.
Arguments:
- concentration: float32 [8, 128, 128, 128], P('sp', 'py', 'pz'), may hold values from -1 to 1.1
- mobility: float32 [8, 8], replicated, may hold values from 0.1 to 0.6
- kappa: float32 [8], replicated, may hold values from 0.5 to 2
- well_depth: float32 [8], P('sp'), may hold values from 0.5 to 2
Outputs:
- updated: float32 [8, 128, 128, 128], P('sp', 'py', 'pz')
All inputs are finite; a program needn't handle non-finite values.
Results may differ from a plain program's by a relative error of at most 0.000084.
Values sent between devices are 32-bit elements; how exact they have to be, the bound alone decides.
A program may use at most 64 MiB of HBM per device.

v0:
```python
import math

import jax
import jax.numpy as jnp
from jax import lax
from jax.sharding import PartitionSpec as P


def tables(count):
    modes = jnp.arange(count, dtype=jnp.int32)
    product = modes[:, None] * modes[None, :] % count
    angle = 2.0 * math.pi * product.astype(jnp.float32) / count
    return (jnp.cos(angle), jnp.sin(angle))


def wave_square(index, count):
    freq = jnp.where(index < count // 2, index, index - count).astype(jnp.float32)
    return (2.0 * math.pi * freq / count) ** 2


def contract(form, values, table):
    return jnp.einsum(form, values, table, precision=lax.Precision.HIGHEST)


def rotate(spectrum, form, count, forward):
    cosine, sine = tables(count)
    real_part, imag_part = (spectrum[0], spectrum[1])
    real_cos = contract(form, real_part, cosine)
    real_sin = contract(form, real_part, sine)
    imag_cos = contract(form, imag_part, cosine)
    imag_sin = contract(form, imag_part, sine)
    if forward:
        return jnp.stack([real_cos + imag_sin, imag_cos - real_sin])
    return jnp.stack([real_cos - imag_sin, imag_cos + real_sin])


def per_device(concentration, mobility, kappa, well_depth):
    local_species, rows_x, rows_y, depth = concentration.shape
    count_sp = lax.axis_size("sp")
    count_py = lax.axis_size("py")
    count_pz = lax.axis_size("pz")
    species = local_species * count_sp
    full_x = rows_x * count_py
    full_y = rows_y * count_pz
    half_depth = depth // 2
    bulk = well_depth[:, None, None, None] * (
        concentration * concentration * concentration - concentration
    )
    fields = jnp.stack([concentration, bulk])
    cosine, sine = tables(depth)
    alternate = (1 - 2 * (jnp.arange(depth, dtype=jnp.int32) % 2)).astype(jnp.float32)
    spectrum = jnp.stack(
        [
            contract("fsxyz,zk->fsxyk", fields, cosine[:, :half_depth]),
            -contract("fsxyz,zk->fsxyk", fields, sine[:, :half_depth]),
        ]
    )
    spectrum = lax.all_to_all(spectrum, "pz", split_axis=5, concat_axis=4, tiled=True)
    own_lines = spectrum.shape[5]
    highest = contract("fsxyz,z->fsxy", fields, alternate)
    highest = lax.all_gather(highest, "pz", axis=3, tiled=True)
    highest = jnp.stack([highest, jnp.zeros_like(highest)])[..., None]
    spectrum = jnp.concatenate([spectrum, highest], axis=5)
    z_modes = jnp.concatenate(
        [
            lax.axis_index("pz") * own_lines + jnp.arange(own_lines, dtype=jnp.int32),
            jnp.full((1,), half_depth, jnp.int32),
        ]
    )
    spectrum = rotate(spectrum, "fsxyz,yk->fsxkz", full_y, True)
    lines = spectrum.shape[5]
    merged = spectrum.reshape(2, 2, local_species * rows_x, full_y, lines)
    merged = lax.all_to_all(merged, ("sp", "py"), split_axis=3, concat_axis=2, tiled=True)
    narrow = merged.shape[3]
    merged = merged.reshape(2, 2, count_sp, count_py, local_species, rows_x, narrow, lines)
    spectrum = merged.transpose(0, 1, 2, 4, 3, 5, 6, 7).reshape(
        2, 2, species, full_x, narrow, lines
    )
    spectrum = rotate(spectrum, "fsxyz,xk->fskyz", full_x, True)
    narrow = spectrum.shape[4]
    lines = spectrum.shape[5]
    y_start = (lax.axis_index("sp") * count_py + lax.axis_index("py")) * narrow
    ksq_x = wave_square(jnp.arange(full_x, dtype=jnp.int32), full_x)
    ksq_y = wave_square(y_start + jnp.arange(narrow, dtype=jnp.int32), full_y)
    ksq_z = wave_square(z_modes, depth)
    ksq = ksq_x[:, None, None] + ksq_y[None, :, None] + ksq_z[None, None, :]
    c_hat = spectrum[:, 0]
    drive = spectrum[:, 1] + kappa[None, :, None, None, None] * ksq[None, None] * c_hat
    mix = jnp.einsum("ij,rjxyz->rixyz", mobility, drive, precision=lax.Precision.HIGHEST)
    stiff = 0.5 * (jnp.diagonal(mobility) * kappa)[:, None, None, None] * (ksq * ksq)[None]
    new_hat = (c_hat * (1.0 + stiff)[None] - 0.5 * ksq[None, None] * mix) / (1.0 + stiff)[None]
    new_hat = rotate(new_hat, "sxyz,xk->skyz", full_x, False)
    ordered = new_hat.reshape(2, count_sp, local_species, count_py, rows_x, narrow, lines)
    ordered = ordered.transpose(0, 1, 3, 2, 4, 5, 6).reshape(2, species * full_x, narrow, lines)
    moved = lax.all_to_all(ordered, ("sp", "py"), split_axis=1, concat_axis=2, tiled=True)
    moved = moved.reshape(2, local_species, rows_x, full_y, lines)
    moved = rotate(moved, "sxyz,yk->sxkz", full_y, False)
    main = moved[..., : lines - 1]
    highest = moved[0, :, :, :, lines - 1]
    main = lax.all_to_all(main, "pz", split_axis=3, concat_axis=4, tiled=True)
    highest = lax.dynamic_slice_in_dim(highest, lax.axis_index("pz") * rows_y, rows_y, 2)
    weight = jnp.where(jnp.arange(half_depth, dtype=jnp.int32) == 0, 1.0, 2.0).astype(jnp.float32)
    result = contract("sxyk,kz->sxyz", main[0] * weight, cosine[:half_depth]) - contract(
        "sxyk,kz->sxyz", main[1] * weight, sine[:half_depth]
    )
    result = result + highest[..., None] * alternate[None, None, None, :]
    return result * (1.0 / (full_x * full_y * depth))


def solution(mesh):
    in_specs = (P("sp", "py", "pz", None), P(), P(), P("sp"))
    out_specs = P("sp", "py", "pz", None)
    return jax.shard_map(
        per_device, mesh=mesh, in_specs=in_specs, out_specs=out_specs, check_vma=False
    )
```

profile of v0, /device:TPU:1, one launch (start us, length us, event | category | flops | bytes accessed | tf_op | source)
XLA Modules:
  0.0 145.5 jit_solution(8476645425575244786)
XLA Ops:
  2.1 1.3 convolution_bitcast_fusion
  3.4 1.3 fusion
  5.6 1.1 reshape.378
  6.8 5.0 %all-to-all-start = ((f32[4,1,16384]{2,1,0:T(1,128)}), f32[4,1,16384]{2,1,0:T(1,128)S(1)}, u32[]{:S(2)}, u32[]{:S(2)}) async-start(f32[4,1,16384]{2,1,0:T(1,128)} %reshape.378), calls=%async_computation | async-start | bytes 524288 | tf_op jit(solution)/shard_map/all_to_all | solution.py:58
  11.8 1.1 fusion.23
  13.0 10.3 %all-gather = f32[2,8,128]{1,0,2:T(2,128)S(1)} all-gather(f32[2,8,32]{1,0,2:T(2,128)S(1)} %bitcast.251), channel_id=2, replica_groups=mesh['sp'=8,'py'=16,'pz'=4] {'pz'}, dimensions={2}, use_global_device_ids=true | all-gather | bytes 10240 | tf_op jit(solution)/shard_map/all_gather | solution.py:61
  23.9 1.4 reduce
  29.5 1.8 %copy.114 = f32[2,2,8,128,17]{4,2,1,0,3:T(8,128)S(1)} copy(f32[2,2,8,128,17]{3,4,2,1,0:T(8,128)S(1)} %maximum_bitcast_fusion) | data formatting | bytes 557056 | tf_op jit(solution)/shard_map/reshape | solution.py:72
  31.3 3.0 %reshape.380 = f32[128,1,544]{2,1,0:T(1,128)} reshape(f32[128,2,2,8,17]{4,3,2,1,0:T(8,128)S(1)} %bitcast.227) | data formatting | bytes 557056
  34.3 22.4 %all-to-all-start.1 = ((f32[128,1,544]{2,1,0:T(1,128)}), f32[128,1,544]{2,1,0:T(1,128)S(1)}, u32[]{:S(2)}, u32[]{:S(2)}) async-start(f32[128,1,544]{2,1,0:T(1,128)} %reshape.380), calls=%async_computation.1 | async-start | bytes 655360 | tf_op jit(solution)/shard_map/all_to_all | solution.py:73
  57.6 24.1 %all-to-all-done.1 = f32[128,1,544]{2,1,0:T(1,128)S(1)} async-done(((f32[128,1,544]{2,1,0:T(1,128)}), f32[128,1,544]{2,1,0:T(1,128)S(1)}, u32[]{:S(2)}, u32[]{:S(2)}) %all-to-all-start.1) | async-done | bytes 278560 | tf_op jit(solution)/shard_map/all_to_all | solution.py:73
  81.7 1.4 reduce.1
  83.1 2.4 %reshape.381 = f32[128,2,2,8,17]{4,3,2,1,0:T(8,128)S(1)} reshape(f32[128,544]{1,0:T(8,128)S(1)} %reduce.1) | data formatting | bytes 557056
  86.0 1.8 %fusion.53 = f32[128,2,8,17]{0,3,2,1:T(8,128)S(1)} fusion(f32[2,8,128,17]{3,2,1,0:T(8,128)S(1)} %bitcast.223), kind=kOutput, calls=%fused_computation.88 | convolution fusion | flops 53706752 | bytes 278528 | tf_op jit(solution)/shard_map/fsxyz,xk->fskyz/dot_general | solution.py:22
  87.8 1.8 %fusion.48 = f32[128,2,8,17]{0,3,2,1:T(8,128)S(1)} fusion(f32[2,8,128,17]{3,2,1,0:T(8,128)S(1)} %bitcast.225), kind=kOutput, calls=%fused_computation.83 | convolution fusion | flops 53706752 | bytes 278528 | tf_op jit(solution)/shard_map/fsxyz,xk->fskyz/dot_general | solution.py:22
  89.6 1.8 %fusion.4 = f32[1,2,8,128,1,17]{3,5,2,1,4,0:T(8,128)S(1)} fusion(f32[128,2,8,17]{0,3,2,1:T(8,128)S(1)} %fusion.53, f32[2,8,128,17]{3,2,1,0:T(8,128)S(1)} %bitcast.226), kind=kOutput, calls=%fused_computation.11 | convolution fusion | flops 53741568 | bytes 417792 | tf_op jit(solution)/shard_map/fsxyz,xk->fskyz/dot_general | solution.py:22
  91.4 1.8 %fusion.3 = f32[1,2,8,128,1,17]{3,5,2,1,4,0:T(8,128)S(1)} fusion(f32[128,2,8,17]{0,3,2,1:T(8,128)S(1)} %fusion.48, f32[2,8,128,17]{3,2,1,0:T(8,128)S(1)} %bitcast.224), kind=kOutput, calls=%fused_computation.9 | convolution fusion | flops 53741568 | bytes 417792 | tf_op jit(solution)/shard_map/fsxyz,xk->fskyz/dot_general | solution.py:22
  96.3 2.5 %reshape.382 = f32[128,1,272]{2,1,0:T(1,128)} reshape(f32[1024,1,2,17]{3,2,1,0:T(2,128)S(1)} %bitcast.230) | data formatting | bytes 278528
  98.9 6.9 %all-to-all-start.2 = ((f32[128,1,272]{2,1,0:T(1,128)}), f32[128,1,272]{2,1,0:T(1,128)S(1)}, u32[]{:S(2)}, u32[]{:S(2)}) async-start(f32[128,1,272]{2,1,0:T(1,128)} %reshape.382), calls=%async_computation.2 | async-start | bytes 393216 | tf_op jit(solution)/shard_map/all_to_all | solution.py:95
  105.9 20.6 %all-to-all-done.2 = f32[128,1,272]{2,1,0:T(1,128)S(1)} async-done(((f32[128,1,272]{2,1,0:T(1,128)}), f32[128,1,272]{2,1,0:T(1,128)S(1)}, u32[]{:S(2)}, u32[]{:S(2)}) %all-to-all-start.2) | async-done | bytes 139296 | tf_op jit(solution)/shard_map/all_to_all | solution.py:95
  127.6 1.7 %reshape.383 = f32[1024,1,2,17]{3,2,1,0:T(2,128)S(1)} reshape(f32[128,272]{1,0:T(8,128)S(1)} %reduce.2) | data formatting | bytes 278528
  133.4 3.4 %all-to-all-start.3 = ((f32[4,1,8192]{2,1,0:T(1,128)}), f32[4,1,8192]{2,1,0:T(1,128)S(1)}, u32[]{:S(2)}, u32[]{:S(2)}) async-start(f32[4,1,8192]{2,1,0:T(1,128)} %reshape.384), calls=%async_computation.3 | async-start | bytes 262144 | tf_op jit(solution)/shard_map/all_to_all | solution.py:100
  136.9 4.8 %all-to-all-done.3 = f32[4,1,8192]{2,1,0:T(1,128)S(1)} async-done(((f32[4,1,8192]{2,1,0:T(1,128)}), f32[4,1,8192]{2,1,0:T(1,128)S(1)}, u32[]{:S(2)}, u32[]{:S(2)}) %all-to-all-start.3) | async-done | bytes 131104 | tf_op jit(solution)/shard_map/all_to_all | solution.py:100
  144.2 1.3 fusion.7
  (66 shorter events, 19.6 us)
Async XLA Ops:
  0.0 56.7 %copy-start = (f32[8,8]{1,0:T(8,128)S(1)}, f32[8,8]{1,0:T(8,128)}, u32[]{:S(2)}) copy-start(f32[8,8]{1,0:T(8,128)} %param.5) | copy-start | bytes 772
  4.7 7.1 %copy-start.1 = (f32[1,8,32,128]{3,2,1,0:T(8,128)S(1)}, f32[1,8,32,128]{3,2,1,0:T(8,128)}, u32[]{:S(2)}) copy-start(f32[1,8,32,128]{3,2,1,0:T(8,128)} %param.4) | copy-start | bytes 393220
  6.8 16.6 %all-to-all-start = ((f32[4,1,16384]{2,1,0:T(1,128)}), f32[4,1,16384]{2,1,0:T(1,128)S(1)}, u32[]{:S(2)}, u32[]{:S(2)}) async-start(f32[4,1,16384]{2,1,0:T(1,128)} %reshape.378), calls=%async_computation | async-start | bytes 524288 | tf_op jit(solution)/shard_map/all_to_all | solution.py:58
  31.3 26.2 %copy-start.2 = (f32[8]{0:T(128)S(1)}, f32[8]{0:T(128)}, u32[]{:S(2)}) copy-start(f32[8]{0:T(128)} %param.6) | copy-start | bytes 100
  34.3 47.4 %all-to-all-start.1 = ((f32[128,1,544]{2,1,0:T(1,128)}), f32[128,1,544]{2,1,0:T(1,128)S(1)}, u32[]{:S(2)}, u32[]{:S(2)}) async-start(f32[128,1,544]{2,1,0:T(1,128)} %reshape.380), calls=%async_computation.1 | async-start | bytes 655360 | tf_op jit(solution)/shard_map/all_to_all | solution.py:73
  98.9 27.6 %all-to-all-start.2 = ((f32[128,1,272]{2,1,0:T(1,128)}), f32[128,1,272]{2,1,0:T(1,128)S(1)}, u32[]{:S(2)}, u32[]{:S(2)}) async-start(f32[128,1,272]{2,1,0:T(1,128)} %reshape.382), calls=%async_computation.2 | async-start | bytes 393216 | tf_op jit(solution)/shard_map/all_to_all | solution.py:95
  133.4 8.2 %all-to-all-start.3 = ((f32[4,1,8192]{2,1,0:T(1,128)}), f32[4,1,8192]{2,1,0:T(1,128)S(1)}, u32[]{:S(2)}, u32[]{:S(2)}) async-start(f32[4,1,8192]{2,1,0:T(1,128)} %reshape.384), calls=%async_computation.3 | async-start | bytes 262144 | tf_op jit(solution)/shard_map/all_to_all | solution.py:100
where the time goes:
time: 146 us
  waiting for transfers between devices  49.4 us (34%)
  starting transfers between devices  37.8 us (26%)
  local copies, waits for them, and re-layouts  20.7 us (14%)
  matrix products  19.4 us (13%)
  blocking collectives  10.3 us (7%)
  other arithmetic  6.83 us (5%)
    all_to_all x1, waiting for transfers between devices, per_device(): lax.all_to_all(merged, ('sp', 'py'), split_axis=3, concat_axis=2, tiled=T...  24.1 us
    all_to_all x1, starting transfers between devices, per_device(): lax.all_to_all(merged, ('sp', 'py'), split_axis=3, concat_axis=2, tiled=T...  22.4 us
    all_to_all x1, waiting for transfers between devices, per_device(): lax.all_to_all(ordered, ('sp', 'py'), split_axis=1, concat_axis=2, tiled=...  20.6 us
    dot_general x21, matrix products, contract(): return jnp.einsum(form, values, table, precision=lax.Precision.HIGHEST)  19.2 us
    unnamed x14, local copies, waits for them, and re-layouts  12.6 us
    all_gather x1, blocking collectives, per_device(): highest = lax.all_gather(highest, 'pz', axis=3, tiled=True)  10.3 us
    all_to_all x1, starting transfers between devices, per_device(): lax.all_to_all(ordered, ('sp', 'py'), split_axis=1, concat_axis=2, tiled=...  6.94 us
    all_to_all x1, starting transfers between devices, per_device(): lax.all_to_all(spectrum, 'pz', split_axis=5, concat_axis=4, tiled=True)  5.01 us
  transfers between devices with their start and end apart: 4, of which 3 were waited for; matrix products, arithmetic and copies ran while one was open for 2% of the time, Pallas kernels for 0%

commit v1 on v0

v1 whole, which is shorter than its diff:
```python
import functools
import math

import jax
import jax.numpy as jnp
import numpy as np
from jax import lax
from jax.experimental import pallas as pl
from jax.experimental.pallas import tpu as pltpu
from jax.sharding import PartitionSpec as P

MESH = pl.DeviceIdType.MESH
N = 128
F32 = jnp.float32
BF16 = jnp.bfloat16


def basis():
    n = np.arange(N)
    out = np.zeros((N, N), np.float64)
    for r in range(N):
        if r == 0:
            out[r] = 1.0 / math.sqrt(N)
        elif r == N // 2:
            out[r] = (1 - 2 * (n % 2)) / math.sqrt(N)
        elif r < N // 2:
            out[r] = np.cos(2 * math.pi * (r * n % N) / N) * math.sqrt(2.0 / N)
        else:
            out[r] = np.sin(2 * math.pi * ((N - r) * n % N) / N) * math.sqrt(2.0 / N)
    return out


def split_table(table):
    table = table.astype(np.float32)
    high = table.astype(BF16)
    low = (table - high.astype(np.float32)).astype(BF16)
    return np.stack([high, low])


def make_tables():
    b = basis()
    y = b.reshape(N, 4, 32)
    fy = np.einsum("kpy,ms->kmpsy", y, np.eye(4)).reshape(512, 512)
    fx = b.reshape(N, 16, 2, 4).transpose(0, 2, 1, 3).reshape(N, N)
    ix = b.T.reshape(16, 2, 4, N).transpose(2, 0, 1, 3).reshape(N, N)
    iy = np.einsum("kpy,ab->paykb", y, np.eye(2)).reshape(256, 256)
    iz = np.broadcast_to(b.reshape(4, 1, 32, N), (4, 4, 32, N)).reshape(512, N)
    return [split_table(t) for t in (b, fy, fx, ix, iy, iz)]


def split(value):
    high = value.astype(BF16)
    return high, (value - high.astype(F32)).astype(BF16)


def dot(a, b, transposed=False):
    dims = (((1,), (1 if transposed else 0,)), ((), ()))
    return lax.dot_general(a, b, dims, preferred_element_type=F32)


def dot3(a, b, transposed=False):
    (ah, al), (bh, bl) = a, b
    return dot(ah, bh, transposed) + (dot(al, bh, transposed) + dot(ah, bl, transposed))


def table(ref):
    return ref[0], ref[1]


def wave(index):
    freq = jnp.where(index < N // 2, index, index - N).astype(F32)
    return (2.0 * math.pi / N * freq) ** 2


def place():
    sp, py = lax.axis_index("sp"), lax.axis_index("py")
    return (sp // 2) * 4 + py // 4, py % 4, sp % 2


def device(z, x, core):
    return {"sp": (z // 4) * 2 + core, "py": (z % 4) * 4 + x}


def offsets():
    order = [8]
    for d in range(7, 0, -1):
        order += [d, 16 - d]
    order += [0]
    return [
        (dz, dx, dc)
        for dz in order
        for dx in (2, 1, 3, 0)
        for dc in (1, 0)
        if (dz, dx, dc) != (0, 0, 0)
    ]


def kernel(
    mob, kap, well, c_hbm, bz_hbm, fy_hbm, fx_hbm, ix_hbm, iy_hbm, iz_hbm, o_ref,
    c, bz, fy, fx, ix, iy, iz, s1, r1, s2, r2, s3, r3, s4, r4, load, send, recv,
):
    z, x, core = place()
    pz = lax.axis_index("pz")
    me = lax.axis_index("sp") * 16 + lax.axis_index("py")
    others = offsets()

    barrier = pltpu.get_barrier_semaphore()
    for k in (1, 2, 3):
        pl.semaphore_signal(barrier, 1, device_id={"pz": (pz + k) % 4}, device_id_type=MESH)
    loads = [
        pltpu.make_async_copy(src, dst, load.at[i])
        for i, (src, dst) in enumerate(
            [(c_hbm, c), (bz_hbm, bz), (fy_hbm, fy), (fx_hbm, fx), (ix_hbm, ix), (iy_hbm, iy), (iz_hbm, iz)]
        )
    ]
    for copy in loads:
        copy.start()

    def peer(offset):
        dz, dx, dc = offset
        return device((z + dz) % 16, (x + dx) % 4, (core + dc) % 2)

    for offset in others:
        pl.semaphore_signal(barrier, 1, device_id=peer(offset), device_id_type=MESH)

    loads[0].wait()
    loads[1].wait()
    conc = c[...].reshape(256, N)
    bulk = well[0] * (conc * conc * conc - conc)
    for f, field in enumerate((conc, bulk)):
        out = dot3(table(bz), split(field), True)
        for p in range(4):
            for h in range(2):
                s1[p, pl.ds(f * 64 + h * 32, 32), :] = out[p * 32 : p * 32 + 32, h * 128 : h * 128 + 128]
    r1[pz] = s1[pz]
    pl.semaphore_wait(barrier, 3 + len(others))
    for k in (2, 1, 3):
        to = (pz + k) % 4
        pltpu.make_async_remote_copy(
            src_ref=s1.at[to], dst_ref=r1.at[pz], send_sem=send.at[0], recv_sem=recv.at[0],
            device_id={"pz": to}, device_id_type=MESH,
        ).start()
    loads[2].wait()
    pltpu.make_async_copy(r1.at[pl.ds(0, 3)], r1.at[pl.ds(0, 3)], recv.at[0]).wait()

    low_high = [split(r1[p]) for p in range(4)]
    high = jnp.concatenate([v[0] for v in low_high], axis=1)
    low = jnp.concatenate([v[1] for v in low_high], axis=1)
    s2[...] = dot3(table(fy), (high, low), True).reshape(N, 4, N)
    r2[me] = s2[me]
    for offset in others:
        to = peer(offset)
        pltpu.make_async_remote_copy(
            src_ref=s2.at[to["sp"] * 16 + to["py"]], dst_ref=r2.at[me], send_sem=send.at[1], recv_sem=recv.at[1],
            device_id=to, device_id_type=MESH,
        ).start()

    lane = lax.broadcasted_iota(jnp.int32, (1, N), 1)
    block = lane // 32

    def lanes(values):
        out = jnp.full((1, N), values[0], F32)
        for q in (1, 2, 3):
            out = jnp.where(block == q, values[q], out)
        return out

    row = lax.broadcasted_iota(jnp.int32, (N, 1), 0)
    ksq = wave(row) + (wave(jnp.full((1, N), me, jnp.int32)) + wave(pz * 32 + lane % 32))
    kappa_ksq = [lanes([kap[4 * h + q] for q in range(4)]) * ksq for h in range(2)]
    factor = []
    for h in range(2):
        stiff = 0.5 * lanes([mob[4 * h + q, 4 * h + q] * kap[4 * h + q] for q in range(4)]) * (ksq * ksq)
        factor.append(0.5 * ksq / (1.0 + stiff))
    coef = [
        [[lanes([mob[4 * hi + q, 4 * hj + (q - s) % 4] for q in range(4)]) for s in range(4)] for hj in range(2)]
        for hi in range(2)
    ]
    loads[3].wait()
    loads[4].wait()
    pltpu.make_async_copy(r2.at[pl.ds(0, 127)], r2.at[pl.ds(0, 127)], recv.at[1]).wait()

    def pick(pieces):
        out = pieces[0]
        for q in (1, 2, 3):
            out = jnp.where(block == q, pieces[q], out)
        return out

    def turn(value, blocks):
        blocks %= 4
        return pltpu.roll(value, blocks * 32, 1) if blocks else value

    hats = [[], []]
    for half in range(2):
        got = [r2[pl.ds((4 * half + q) * 16, 16)].reshape(64, N) for q in range(4)]
        for f in range(2):
            rows = [pick([turn(got[q], q - (2 * f + h)) for q in range(4)]) for h in range(2)]
            hats[f].append(dot3(table(fx), split(jnp.concatenate(rows, axis=0))))
    drive = [hats[1][h] + kappa_ksq[h] * hats[0][h] for h in range(2)]
    turned = [[turn(drive[h], s) for s in range(4)] for h in range(2)]
    for half in range(2):
        mix = sum(coef[half][h][s] * turned[h][s] for h in range(2) for s in range(4))
        new = hats[0][half] - factor[half] * mix
        out = dot3(table(ix), split(new))
        for q in range(4):
            back = pick([turn(out[m * 32 : m * 32 + 32], m - q) for m in range(4)])
            s3[pl.ds((4 * half + q) * 16, 16)] = back.reshape(16, 2, N)
    r3[me] = s3[me]
    for offset in others:
        to = peer(offset)
        pltpu.make_async_remote_copy(
            src_ref=s3.at[to["sp"] * 16 + to["py"]], dst_ref=r3.at[me], send_sem=send.at[2], recv_sem=recv.at[2],
            device_id=to, device_id_type=MESH,
        ).start()
    loads[5].wait()
    loads[6].wait()
    pltpu.make_async_copy(r3.at[pl.ds(0, 127)], r3.at[pl.ds(0, 127)], recv.at[2]).wait()

    s4[...] = dot3(table(iy), split(r3[...].reshape(256, N))).reshape(4, 64, N)
    r4[pz] = s4[pz]
    for k in (2, 1, 3):
        to = (pz + k) % 4
        pltpu.make_async_remote_copy(
            src_ref=s4.at[to], dst_ref=r4.at[pz], send_sem=send.at[3], recv_sem=recv.at[3],
            device_id={"pz": to}, device_id_type=MESH,
        ).start()
    pltpu.make_async_copy(r4.at[pl.ds(0, 3)], r4.at[pl.ds(0, 3)], recv.at[3]).wait()

    lanes4 = jnp.concatenate([r4[p] for p in range(4)], axis=1)
    spot = lax.broadcasted_iota(jnp.int32, (1, 512), 1) // 32 % 4
    masked = jnp.concatenate([jnp.where(spot == m, lanes4, 0.0) for m in range(4)], axis=0)
    out = dot3(split(masked), table(iz))
    for m in range(4):
        for h in range(2):
            o_ref[h * 4 + m] = out[m * 64 + h * 32 : m * 64 + h * 32 + 32, :]

    pltpu.make_async_copy(s1.at[pl.ds(0, 3)], s1.at[pl.ds(0, 3)], send.at[0]).wait()
    pltpu.make_async_copy(s2.at[pl.ds(0, 127)], s2.at[pl.ds(0, 127)], send.at[1]).wait()
    pltpu.make_async_copy(s3.at[pl.ds(0, 127)], s3.at[pl.ds(0, 127)], send.at[2]).wait()
    pltpu.make_async_copy(s4.at[pl.ds(0, 3)], s4.at[pl.ds(0, 3)], send.at[3]).wait()


def per_device(concentration, mobility, kappa, well_depth):
    tables = make_tables()
    smem = pl.BlockSpec(memory_space=pltpu.SMEM)
    hbm = pl.BlockSpec(memory_space=pl.ANY)
    out = pl.pallas_call(
        kernel,
        out_shape=jax.ShapeDtypeStruct((8, 32, N), F32),
        in_specs=[smem] * 3 + [hbm] * 7,
        out_specs=pl.BlockSpec(memory_space=pltpu.VMEM),
        scratch_shapes=[
            pltpu.VMEM((8, 32, N), F32),
            *[pltpu.VMEM(t.shape, BF16) for t in tables],
            pltpu.VMEM((4, N, N), F32),
            pltpu.VMEM((4, N, N), F32),
            pltpu.VMEM((N, 4, N), F32),
            pltpu.VMEM((N, 4, N), F32),
            pltpu.VMEM((N, 2, N), F32),
            pltpu.VMEM((N, 2, N), F32),
            pltpu.VMEM((4, 64, N), F32),
            pltpu.VMEM((4, 64, N), F32),
            pltpu.SemaphoreType.DMA((7,)),
            pltpu.SemaphoreType.DMA((4,)),
            pltpu.SemaphoreType.DMA((4,)),
        ],
        compiler_params=pltpu.CompilerParams(collective_id=0, has_side_effects=True),
    )(mobility, kappa, well_depth, concentration[0], *[jnp.asarray(t) for t in tables])
    return out[None]


def solution(mesh):
    in_specs = (P("sp", "py", "pz", None), P(), P(), P("sp"))
    out_specs = P("sp", "py", "pz", None)
    return jax.shard_map(
        per_device, mesh=mesh, in_specs=in_specs, out_specs=out_specs, check_vma=False
    )
```

time: 146 us -> 57.8 us (0.40)
  Pallas kernels: 0 us -> 55.5 us
  waiting for transfers between devices: 49.4 us -> 0 us
  starting transfers between devices: 37.8 us -> 0 us
  matrix products: 19.4 us -> 0 us
  local copies, waits for them, and re-layouts: 20.7 us -> 1.57 us
  blocking collectives: 10.3 us -> 0 us
  other arithmetic: 6.83 us -> 0 us
    pallas_call x0 -> x1, Pallas kernels: none -> 55.5 us  [per_device(): pl.pallas_call(kernel, out_shape=jax.ShapeDtypeStruct((8, 32, N), F32), i...]
    all_to_all x4 -> x0, waiting for transfers between devices: 49.4 us -> none  [the longest x1 24.1 us: per_device(): lax.all_to_all(merged, ('sp', 'py'), split_axis=3, concat_axis=2, tiled=T...]
    all_to_all x4 -> x0, starting transfers between devices: 37.8 us -> none  [the longest x1 22.4 us: per_device(): lax.all_to_all(merged, ('sp', 'py'), split_axis=3, concat_axis=2, tiled=T...]
    dot_general x22 -> x0, matrix products: 19.4 us -> none  [the longest x21 19.2 us: contract(): return jnp.einsum(form, values, table, precision=lax.Precision.HIGHEST)]
    unnamed x14 -> x1, local copies, waits for them, and re-layouts: 12.6 us -> 1.57 us
    all_gather x1 -> x0, blocking collectives: 10.3 us -> none  [per_device(): highest = lax.all_gather(highest, 'pz', axis=3, tiled=True)]
    all_to_all x4 -> x0, other arithmetic: 4.82 us -> none  [the longest x1 1.4 us: per_device(): lax.all_to_all(merged, ('sp', 'py'), split_axis=3, concat_axis=2, tiled=T...]
    all_to_all x7 -> x0, local copies, waits for them, and re-layouts: 3.26 us -> none  [the longest x4 2.1 us: per_device(): lax.all_to_all(spectrum, 'pz', split_axis=5, concat_axis=4, tiled=True)]
  transfers between devices with their start and end apart: 4 -> 0, of which waited for: 3 -> 0; matrix products, arithmetic and copies ran while one was open for 2% -> 0% of each run, Pallas kernels for 0% -> 0%
where the time goes in v1:
time: 57.8 us; the launch traced here: 57.7 us
  Pallas kernels  55.5 us (96%)
  local copies, waits for them, and re-layouts  1.57 us (3%)
  between operations  0.66 us (1%)
    pallas_call x1, Pallas kernels, per_device(): pl.pallas_call(kernel, out_shape=jax.ShapeDtypeStruct((8, 32, N), F32), i...  55.5 us
    unnamed x1, local copies, waits for them, and re-layouts  1.57 us

profile of v1, /device:TPU:1, one launch (start us, length us, event | category | flops | bytes accessed | tf_op | source)
XLA Modules:
  0.0 57.7 jit_solution(15533613416875467237)
XLA Ops:
  0.7 55.5 %shard_map.100 = f32[8,32,128]{2,1,0:T(8,128)} custom-call(f32[8,8]{1,0:T(8,128)} %mob.1, f32[8]{0:T(128)} %kap.1, f32[1]{0:T(128)S(6)} %copy.12.well, f32[8,32,128]{2,1,0:T(8,128)} %bitcast.3, bf16[2,128,128]{2,1,0:T(8,128)(2,1)} %constant.12.clone.bz_hbm, bf16[2,512,512]{2,1,0:T(8,128)(2,1)} %constant.13.clone.fy_hbm, ...), custom_call_target="tpu_custom_call" | custom-call | tf_op jit(solution)/shard_map/pallas_call | solution.py:246
  56.1 1.6 %copy.13 = f32[1,8,32,128]{3,2,1,0:T(8,128)} copy(f32[1,8,32,128]{3,2,1,0:T(8,128)} %bitcast.2) | data formatting | bytes 262144

commit v2 on v1

v2 whole, which is shorter than its diff:
```python
import functools
import math

import jax
import jax.numpy as jnp
import numpy as np
from jax import lax
from jax.experimental import pallas as pl
from jax.experimental.pallas import tpu as pltpu
from jax.sharding import PartitionSpec as P

MESH = pl.DeviceIdType.MESH
N = 128
F32 = jnp.float32
BF16 = jnp.bfloat16
LINE = [8, 7, 9, 6, 10, 5, 11, 4, 12, 3, 13, 2, 14, 1, 15]


def basis():
    n = np.arange(N)
    out = np.zeros((N, N), np.float64)
    for r in range(N):
        if r == 0:
            out[r] = 1.0 / math.sqrt(N)
        elif r == N // 2:
            out[r] = (1 - 2 * (n % 2)) / math.sqrt(N)
        elif r < N // 2:
            out[r] = np.cos(2 * math.pi * (r * n % N) / N) * math.sqrt(2.0 / N)
        else:
            out[r] = np.sin(2 * math.pi * ((N - r) * n % N) / N) * math.sqrt(2.0 / N)
    return out


def split_table(table):
    table = table.astype(np.float32)
    high = table.astype(BF16)
    low = (table - high.astype(np.float32)).astype(BF16)
    return np.stack([high, low])


def make_tables():
    b = basis()
    y = b.reshape(N, 4, 32)
    fy = np.einsum("kpy,ed,g->kepgdy", y, np.eye(2), np.ones(2)).reshape(256, 512)
    fx = b.reshape(N, 16, 2, 2, 2).transpose(0, 3, 2, 1, 4).reshape(N, N)
    ix = b.T.reshape(16, 8, N).transpose(1, 0, 2).reshape(N, N)
    iz = b.reshape(4, 2, 16, N).transpose(1, 0, 2, 3).reshape(N, N)
    return [split_table(t) for t in (b, fy, fx, ix, b.T, iz)]


def split(value):
    high = value.astype(BF16)
    return high, (value - high.astype(F32)).astype(BF16)


def dot(a, b, transposed=False):
    dims = (((1,), (1 if transposed else 0,)), ((), ()))
    return lax.dot_general(a, b, dims, preferred_element_type=F32)


def dot3(a, b, transposed=False):
    (ah, al), (bh, bl) = a, b
    return dot(ah, bh, transposed) + (dot(al, bh, transposed) + dot(ah, bl, transposed))


def table(ref):
    return ref[0], ref[1]


def wave(index):
    freq = jnp.where(index < N // 2, index, index - N).astype(F32)
    return (2.0 * math.pi / N * freq) ** 2


def place():
    sp, py = lax.axis_index("sp"), lax.axis_index("py")
    return (sp // 2) * 4 + py // 4, py % 4, sp % 2


def device(z, x, core):
    return {"sp": (z // 4) * 2 + core, "py": (z % 4) * 4 + x}


def offsets():
    return [
        (dz, dx, dc)
        for dz in LINE + [0]
        for dx in (2, 1, 3, 0)
        for dc in (1, 0)
        if (dz, dx, dc) != (0, 0, 0)
    ]


def swap_blocks(values):
    block = lax.broadcasted_iota(jnp.int32, (1, N), 1) // 16
    values = list(values)
    for d in (1, 2, 4):
        low = block // d % 2 == 0
        for i in range(8):
            if i // d % 2 == 0:
                a, b = values[i], values[i + d]
                values[i] = jnp.where(low, a, pltpu.roll(b, 16 * d, 1))
                values[i + d] = jnp.where(low, pltpu.roll(a, N - 16 * d, 1), b)
    return values


def kernel(
    mob, kap, well, c_hbm, bz_hbm, fy_hbm, fx_hbm, ix_hbm, iy_hbm, iz_hbm, o_ref,
    c, bz, fy, fx, ix, iy, iz, s1, r1, s2, r2, s3, r3, s4, r4, load, send, recv, chain,
):
    z, x, core = place()
    pz = lax.axis_index("pz")
    me = lax.axis_index("sp") * 16 + lax.axis_index("py")
    others = offsets()
    barrier = pltpu.get_barrier_semaphore()

    def signal(sem, to):
        pl.semaphore_signal(sem, 1, device_id=to, device_id_type=MESH)

    def peer(offset):
        dz, dx, dc = offset
        return device((z + dz) % 16, (x + dx) % 4, (core + dc) % 2)

    plane = [offset for offset in others if offset[0] == 0]

    for k in (2, 1, 3):
        signal(barrier, {"pz": (pz + k) % 4})
    for dz in LINE:
        signal(barrier, peer((dz, 0, 0)))
    for offset in plane:
        signal(barrier, peer(offset))
    loads = [
        pltpu.make_async_copy(src, dst, load.at[i])
        for i, (src, dst) in enumerate(
            [(c_hbm, c), (bz_hbm, bz), (fy_hbm, fy), (fx_hbm, fx), (ix_hbm, ix), (iy_hbm, iy), (iz_hbm, iz)]
        )
    ]
    for copy in loads:
        copy.start()

    def near(i, src, dst):
        for k in (2, 1, 3):
            to = (pz + k) % 4
            pltpu.make_async_remote_copy(
                src_ref=src.at[to], dst_ref=dst.at[pz], send_sem=send.at[i], recv_sem=recv.at[i],
                device_id={"pz": to}, device_id_type=MESH,
            ).start()

    def far(i, src, dst):
        for offset in others:
            to = peer(offset)
            pltpu.make_async_remote_copy(
                src_ref=src.at[to["sp"] * 16 + to["py"]], dst_ref=dst.at[me],
                send_sem=send.at[i], recv_sem=recv.at[i], device_id=to, device_id_type=MESH,
            ).start()

    def arrive(ref, sem):
        pltpu.make_async_copy(ref, ref, sem).wait()

    loads[0].wait()
    loads[1].wait()
    conc = c[...].reshape(256, N)
    bulk = well[0] * (conc * conc * conc - conc)
    for f, field in enumerate((conc, bulk)):
        out = dot3(table(bz), split(field), True)
        for p in range(4):
            for half in range(2):
                for h in range(2):
                    at = p * 32 + half * 16
                    s1[half, p, pl.ds(f * 32 + h * 16, 16), :] = out[at : at + 16, h * 128 : h * 128 + 128]
    pl.semaphore_wait(barrier, 25)
    for half in range(2):
        near(half, s1.at[half], r1.at[half])
    for offset in plane:
        signal(chain, peer(offset))
    for half in range(2):
        r1[half, pz] = s1[half, pz]
    loads[2].wait()

    left = lax.broadcasted_iota(jnp.int32, (1, N), 1) < 64
    for half in range(2):
        arrive(r1.at[half, pl.ds(0, 3)], recv.at[half])
        parts = []
        for p in range(4):
            value = r1[half, p]
            parts.append(split(jnp.concatenate([jnp.where(left, value, 0.0), jnp.where(left, 0.0, value)], axis=0)))
        both = [jnp.concatenate([v[i] for v in parts], axis=1) for i in range(2)]
        s2[half] = dot3(table(fy), both, True).reshape(N, 2, N)
        if half == 0:
            pl.semaphore_wait(chain, 7)
        far(2 + half, s2.at[half], r2.at[half])
        r2[half, me] = s2[half, me]

    lane = lax.broadcasted_iota(jnp.int32, (1, N), 1)
    block = lane // 16

    def lanes(values):
        out = jnp.full((1, N), values[0], F32)
        for q in range(1, 8):
            out = jnp.where(block == q, values[q], out)
        return out

    row = lax.broadcasted_iota(jnp.int32, (N, 1), 0)
    ksq_xy = wave(row) + wave(jnp.full((1, N), me, jnp.int32))
    kappa = lanes([kap[j] for j in range(8)])
    self_kappa = lanes([mob[j, j] * kap[j] for j in range(8)])
    coef = [lanes([mob[q, (q - s) % 8] for q in range(8)]) for s in range(8)]
    kappa_ksq, factor = [], []
    for half in range(2):
        ksq = ksq_xy + wave(pz * 32 + half * 16 + lane % 16)
        kappa_ksq.append(kappa * ksq)
        factor.append(0.5 * ksq / (1.0 + 0.5 * self_kappa * (ksq * ksq)))
    loads[3].wait()
    loads[4].wait()

    for half in range(2):
        arrive(r2.at[half, pl.ds(0, 127)], recv.at[2 + half])
        got = swap_blocks([r2[half, pl.ds(j * 16, 16)].reshape(32, N) for j in range(8)])
        c_hat, bulk_hat = [
            dot3(table(fx), split(jnp.concatenate([got[g * 4 + f * 2 + h] for g in range(2) for h in range(2)], axis=0)))
            for f in range(2)
        ]
        drive = bulk_hat + kappa_ksq[half] * c_hat
        mix = coef[0] * drive
        for s in range(1, 8):
            mix = mix + coef[s] * pltpu.roll(drive, 16 * s, 1)
        out = dot3(table(ix), split(c_hat - factor[half] * mix))
        back = swap_blocks([out[i * 16 : i * 16 + 16] for i in range(8)])
        for i in range(8):
            s3[half, pl.ds(i * 16, 16)] = back[i].reshape(16, 1, N)
        far(4 + half, s3.at[half], r3.at[half])
        r3[half, me] = s3[half, me]
    loads[5].wait()
    loads[6].wait()

    for half in range(2):
        arrive(r3.at[half, pl.ds(0, 127)], recv.at[4 + half])
        s4[half] = dot3(table(iy), split(r3[half].reshape(N, N))).reshape(4, 32, N)
        near(6 + half, s4.at[half], r4.at[half])
        r4[half, pz] = s4[half, pz]

    for half in range(2):
        arrive(r4.at[half, pl.ds(0, 3)], recv.at[6 + half])
    rows = swap_blocks([r4[half, p] for half in range(2) for p in range(4)])
    out = dot3(split(jnp.concatenate(rows, axis=0)), table(iz))
    o_ref[...] = out.reshape(8, 32, N)

    for half in range(2):
        arrive(s1.at[half, pl.ds(0, 3)], send.at[half])
        arrive(s2.at[half, pl.ds(0, 127)], send.at[2 + half])
        arrive(s3.at[half, pl.ds(0, 127)], send.at[4 + half])
        arrive(s4.at[half, pl.ds(0, 3)], send.at[6 + half])


def per_device(concentration, mobility, kappa, well_depth):
    tables = make_tables()
    smem = pl.BlockSpec(memory_space=pltpu.SMEM)
    hbm = pl.BlockSpec(memory_space=pltpu.HBM)
    in_hbm = [
        pltpu.with_memory_space_constraint(v, pltpu.HBM)
        for v in (mobility, kappa, concentration[0], *map(jnp.asarray, tables))
    ]
    out = pl.pallas_call(
        kernel,
        out_shape=jax.ShapeDtypeStruct((8, 32, N), F32),
        in_specs=[smem] * 3 + [hbm] * 7,
        out_specs=pl.BlockSpec(memory_space=pltpu.VMEM),
        scratch_shapes=[
            pltpu.VMEM((8, 32, N), F32),
            *[pltpu.VMEM(t.shape, BF16) for t in tables],
            pltpu.VMEM((2, 4, 64, N), F32),
            pltpu.VMEM((2, 4, 64, N), F32),
            pltpu.VMEM((2, N, 2, N), F32),
            pltpu.VMEM((2, N, 2, N), F32),
            pltpu.VMEM((2, N, 1, N), F32),
            pltpu.VMEM((2, N, 1, N), F32),
            pltpu.VMEM((2, 4, 32, N), F32),
            pltpu.VMEM((2, 4, 32, N), F32),
            pltpu.SemaphoreType.DMA((7,)),
            pltpu.SemaphoreType.DMA((8,)),
            pltpu.SemaphoreType.DMA((8,)),
            pltpu.SemaphoreType.REGULAR,
        ],
        compiler_params=pltpu.CompilerParams(
            collective_id=0, has_side_effects=True, vmem_limit_bytes=12 * 2**20
        ),
    )(in_hbm[0], in_hbm[1], well_depth, *in_hbm[2:])
    return out[None]


def solution(mesh):
    in_specs = (P("sp", "py", "pz", None), P(), P(), P("sp"))
    out_specs = P("sp", "py", "pz", None)
    return jax.shard_map(
        per_device, mesh=mesh, in_specs=in_specs, out_specs=out_specs, check_vma=False
    )
```

time: 57.8 us -> 51.1 us (0.88)
  Pallas kernels: 55.5 us -> 49.6 us
  local copies, waits for them, and re-layouts: 1.57 us -> 0.66 us
    pallas_call x1, Pallas kernels: 55.5 us -> 49.6 us  [per_device(): pl.pallas_call(kernel, out_shape=jax.ShapeDtypeStruct((8, 32, N), F32), i...]
    unnamed x1, local copies, waits for them, and re-layouts: 1.57 us -> 0.66 us
where the time goes in v2:
time: 51.1 us; the launch traced here: 50.9 us
  Pallas kernels  49.6 us (97%)
  local copies, waits for them, and re-layouts  0.66 us (1%)
  between operations  0.66 us (1%)
    pallas_call x1, Pallas kernels, per_device(): pl.pallas_call(kernel, out_shape=jax.ShapeDtypeStruct((8, 32, N), F32), i...  49.6 us

profile of v2, /device:TPU:1, one launch (start us, length us, event | category | flops | bytes accessed | tf_op | source)
XLA Modules:
  0.0 50.9 jit_solution(11538619060689090598)
XLA Ops:
  0.7 49.6 %shard_map.100 = f32[8,32,128]{2,1,0:T(8,128)S(1)} custom-call(f32[8,8]{1,0:T(8,128)} %mob.1, f32[8]{0:T(128)} %kap.1, f32[1]{0:T(128)S(6)} %copy.12.well, f32[8,32,128]{2,1,0:T(8,128)} %bitcast.3, bf16[2,128,128]{2,1,0:T(8,128)(2,1)} %constant.12.clone.bz_hbm, bf16[2,256,512]{2,1,0:T(8,128)(2,1)} %constant.13.clone.fy_hbm, ...), custom_call_target="tpu_custom_call" | custom-call | tf_op jit(solution)/shard_map/pallas_call | solution.py:263
  50.3 0.7 %copy.13 = f32[1,8,32,128]{3,2,1,0:T(8,128)} copy(f32[1,8,32,128]{3,2,1,0:T(8,128)S(1)} %bitcast.2) | data formatting | bytes 262144

commit v3 on v2

--- a/solution.py
+++ b/solution.py
@@ -105,8 +105,8 @@
 
 
 def kernel(
-    mob, kap, well, c_hbm, bz_hbm, fy_hbm, fx_hbm, ix_hbm, iy_hbm, iz_hbm, o_ref,
-    c, bz, fy, fx, ix, iy, iz, s1, r1, s2, r2, s3, r3, s4, r4, load, send, recv, chain,
+    c_hbm, bz_hbm, fy_hbm, fx_hbm, ix_hbm, iy_hbm, iz_hbm, mob_hbm, kap_hbm, well, o_ref,
+    c, bz, fy, fx, ix, iy, iz, mob, kap, s1, r1, s2, r2, s3, r3, s4, r4, load, send, recv, chain,
 ):
     z, x, core = place()
     pz = lax.axis_index("pz")
@@ -123,16 +123,19 @@
 
     plane = [offset for offset in others if offset[0] == 0]
 
+    for dz in LINE:
+        signal(barrier, peer((dz, 0, 0)))
     for k in (2, 1, 3):
         signal(barrier, {"pz": (pz + k) % 4})
-    for dz in LINE:
-        signal(barrier, peer((dz, 0, 0)))
     for offset in plane:
         signal(barrier, peer(offset))
     loads = [
         pltpu.make_async_copy(src, dst, load.at[i])
         for i, (src, dst) in enumerate(
-            [(c_hbm, c), (bz_hbm, bz), (fy_hbm, fy), (fx_hbm, fx), (ix_hbm, ix), (iy_hbm, iy), (iz_hbm, iz)]
+            [
+                (c_hbm, c), (bz_hbm, bz), (fy_hbm, fy), (fx_hbm, fx), (ix_hbm, ix), (iy_hbm, iy), (iz_hbm, iz),
+                (mob_hbm, mob), (kap_hbm, kap),
+            ]
         )
     ]
     for copy in loads:
@@ -200,6 +203,8 @@
             out = jnp.where(block == q, values[q], out)
         return out
 
+    loads[7].wait()
+    loads[8].wait()
     row = lax.broadcasted_iota(jnp.int32, (N, 1), 0)
     ksq_xy = wave(row) + wave(jnp.full((1, N), me, jnp.int32))
     kappa = lanes([kap[j] for j in range(8)])
@@ -254,20 +259,21 @@
 
 def per_device(concentration, mobility, kappa, well_depth):
     tables = make_tables()
-    smem = pl.BlockSpec(memory_space=pltpu.SMEM)
     hbm = pl.BlockSpec(memory_space=pltpu.HBM)
     in_hbm = [
         pltpu.with_memory_space_constraint(v, pltpu.HBM)
-        for v in (mobility, kappa, concentration[0], *map(jnp.asarray, tables))
+        for v in (concentration[0], *map(jnp.asarray, tables), mobility, kappa)
     ]
     out = pl.pallas_call(
         kernel,
         out_shape=jax.ShapeDtypeStruct((8, 32, N), F32),
-        in_specs=[smem] * 3 + [hbm] * 7,
+        in_specs=[hbm] * 9 + [pl.BlockSpec(memory_space=pltpu.SMEM)],
         out_specs=pl.BlockSpec(memory_space=pltpu.VMEM),
         scratch_shapes=[
             pltpu.VMEM((8, 32, N), F32),
             *[pltpu.VMEM(t.shape, BF16) for t in tables],
+            pltpu.SMEM((8, 8), F32),
+            pltpu.SMEM((8,), F32),
             pltpu.VMEM((2, 4, 64, N), F32),
             pltpu.VMEM((2, 4, 64, N), F32),
             pltpu.VMEM((2, N, 2, N), F32),
@@ -276,7 +282,7 @@
             pltpu.VMEM((2, N, 1, N), F32),
             pltpu.VMEM((2, 4, 32, N), F32),
             pltpu.VMEM((2, 4, 32, N), F32),
-            pltpu.SemaphoreType.DMA((7,)),
+            pltpu.SemaphoreType.DMA((10,)),
             pltpu.SemaphoreType.DMA((8,)),
             pltpu.SemaphoreType.DMA((8,)),
             pltpu.SemaphoreType.REGULAR,
@@ -284,7 +290,7 @@
         compiler_params=pltpu.CompilerParams(
             collective_id=0, has_side_effects=True, vmem_limit_bytes=12 * 2**20
         ),
-    )(in_hbm[0], in_hbm[1], well_depth, *in_hbm[2:])
+    )(*in_hbm, well_depth)
     return out[None]
 
 

time: 51.1 us -> 50.3 us (0.984)
  Pallas kernels: 49.6 us -> 48.9 us
    pallas_call x1, Pallas kernels: 49.6 us -> 48.9 us  [per_device(): pl.pallas_call(kernel, out_shape=jax.ShapeDtypeStruct((8, 32, N), F32), i...]
where the time goes in v3:
time: 50.3 us; the launch traced here: 50.2 us
  Pallas kernels  48.9 us (97%)
  local copies, waits for them, and re-layouts  0.66 us (1%)
  between operations  0.66 us (1%)
    pallas_call x1, Pallas kernels, per_device(): pl.pallas_call(kernel, out_shape=jax.ShapeDtypeStruct((8, 32, N), F32), i...  48.9 us

profile of v3, /device:TPU:1, one launch (start us, length us, event | category | flops | bytes accessed | tf_op | source)
XLA Modules:
  0.0 50.2 jit_solution(13437586476973384132)
XLA Ops:
  0.7 48.9 %shard_map.100 = f32[8,32,128]{2,1,0:T(8,128)S(1)} custom-call(f32[8,32,128]{2,1,0:T(8,128)} %bitcast.3, bf16[2,128,128]{2,1,0:T(8,128)(2,1)} %constant.12.clone.bz_hbm, bf16[2,256,512]{2,1,0:T(8,128)(2,1)} %constant.13.clone.fy_hbm, bf16[2,128,128]{2,1,0:T(8,128)(2,1)} %constant.14.clone.fx_hbm, bf16[2,128,128]{2,1,0:T(8,128)(2,1)} %constant.15.clone.ix_hbm, ...), custom_call_target="tpu_custom_call" | custom-call | tf_op jit(solution)/shard_map/pallas_call | solution.py:267
  49.5 0.7 %copy.13 = f32[1,8,32,128]{3,2,1,0:T(8,128)} copy(f32[1,8,32,128]{3,2,1,0:T(8,128)S(1)} %bitcast.2) | data formatting | bytes 262144

commit v4 on v3

--- a/solution.py
+++ b/solution.py
@@ -106,7 +106,7 @@
 
 def kernel(
     c_hbm, bz_hbm, fy_hbm, fx_hbm, ix_hbm, iy_hbm, iz_hbm, mob_hbm, kap_hbm, well, o_ref,
-    c, bz, fy, fx, ix, iy, iz, mob, kap, s1, r1, s2, r2, s3, r3, s4, r4, load, send, recv, chain,
+    c, bz, fy, fx, ix, iy, iz, mob, kap, s1, r1, s2, r2, s3, r3, s4, r4, load, send, recv, chain, ready,
 ):
     z, x, core = place()
     pz = lax.axis_index("pz")
@@ -123,12 +123,6 @@
 
     plane = [offset for offset in others if offset[0] == 0]
 
-    for dz in LINE:
-        signal(barrier, peer((dz, 0, 0)))
-    for k in (2, 1, 3):
-        signal(barrier, {"pz": (pz + k) % 4})
-    for offset in plane:
-        signal(barrier, peer(offset))
     loads = [
         pltpu.make_async_copy(src, dst, load.at[i])
         for i, (src, dst) in enumerate(
@@ -141,6 +135,13 @@
     for copy in loads:
         copy.start()
 
+    for dz in LINE:
+        signal(barrier, device((z + dz) % 16, x, 0))
+    for k in (2, 1, 3):
+        signal(barrier, {"pz": (pz + k) % 4, **device(z, x, 1)})
+    signal(barrier, device(z, x, 1 - core))
+    for dx in (2, 1, 3):
+        signal(barrier, device(z, (x + dx) % 4, 0))
     def near(i, src, dst):
         for k in (2, 1, 3):
             to = (pz + k) % 4
@@ -171,13 +172,26 @@
                 for h in range(2):
                     at = p * 32 + half * 16
                     s1[half, p, pl.ds(f * 32 + h * 16, 16), :] = out[at : at + 16, h * 128 : h * 128 + 128]
-    pl.semaphore_wait(barrier, 25)
+    @pl.when(core == 1)
+    def _():
+        pl.semaphore_wait(barrier, 7)
+        signal(ready, device(z, x, 0))
+
+    @pl.when(core == 0)
+    def _():
+        pl.semaphore_wait(ready, 1)
+
     for half in range(2):
         near(half, s1.at[half], r1.at[half])
-    for offset in plane:
-        signal(chain, peer(offset))
     for half in range(2):
         r1[half, pz] = s1[half, pz]
+
+    @pl.when(core == 0)
+    def _():
+        pl.semaphore_wait(barrier, 37)
+        for offset in plane:
+            signal(chain, peer(offset))
+
     loads[2].wait()
 
     left = lax.broadcasted_iota(jnp.int32, (1, N), 1) < 64
@@ -190,7 +204,7 @@
         both = [jnp.concatenate([v[i] for v in parts], axis=1) for i in range(2)]
         s2[half] = dot3(table(fy), both, True).reshape(N, 2, N)
         if half == 0:
-            pl.semaphore_wait(chain, 7)
+            pl.semaphore_wait(chain, jnp.where(core == 0, 3, 4))
         far(2 + half, s2.at[half], r2.at[half])
         r2[half, me] = s2[half, me]
 
@@ -286,6 +300,7 @@
             pltpu.SemaphoreType.DMA((8,)),
             pltpu.SemaphoreType.DMA((8,)),
             pltpu.SemaphoreType.REGULAR,
+            pltpu.SemaphoreType.REGULAR,
         ],
         compiler_params=pltpu.CompilerParams(
             collective_id=0, has_side_effects=True, vmem_limit_bytes=12 * 2**20

time: 50.3 us -> 50.2 us (level)
  no operation moved by 1% of the time
where the time goes in v4:
time: 50.2 us; the launch traced here: 50 us
  Pallas kernels  48.7 us (97%)
  local copies, waits for them, and re-layouts  0.66 us (1%)
  between operations  0.66 us (1%)
    pallas_call x1, Pallas kernels, per_device(): pl.pallas_call(kernel, out_shape=jax.ShapeDtypeStruct((8, 32, N), F32), i...  48.7 us

profile of v4, /device:TPU:1, one launch (start us, length us, event | category | flops | bytes accessed | tf_op | source)
XLA Modules:
  0.0 50.0 jit_solution(16372106876427512048)
XLA Ops:
  0.7 48.7 %shard_map.100 = f32[8,32,128]{2,1,0:T(8,128)S(1)} custom-call(f32[8,32,128]{2,1,0:T(8,128)} %bitcast.3, bf16[2,128,128]{2,1,0:T(8,128)(2,1)} %constant.12.clone.bz_hbm, bf16[2,256,512]{2,1,0:T(8,128)(2,1)} %constant.13.clone.fy_hbm, bf16[2,128,128]{2,1,0:T(8,128)(2,1)} %constant.14.clone.fx_hbm, bf16[2,128,128]{2,1,0:T(8,128)(2,1)} %constant.15.clone.ix_hbm, ...), custom_call_target="tpu_custom_call" | custom-call | tf_op jit(solution)/shard_map/pallas_call | solution.py:281
  49.4 0.7 %copy.13 = f32[1,8,32,128]{3,2,1,0:T(8,128)} copy(f32[1,8,32,128]{3,2,1,0:T(8,128)S(1)} %bitcast.2) | data formatting | bytes 262144
